TPU v7x, 32 devices: a whole 2x2x4 slice. The times are simulated.
32 devices in a mesh: head: 2 (over x), inner: 4 (over y, core), outer: 4 (over z).
Axes of the slice: x: 2, y: 2, z: 4, core: 2. Of those that a mesh axis runs over, the one named last changes fastest.
Arguments:
- queries: float32 [2048, 8, 128], P(('inner', 'outer'), 'head'), may hold values from -8 to 8
- key_rows: float32 [2048, 128], P(('inner', 'outer'), 'head'), may hold values from -8 to 8
- values: float32 [2048, 128], P(('inner', 'outer'), 'head'), may hold values from -24 to 24
- out_grad: float32 [2048, 8, 128], P(('inner', 'outer'), 'head'), may hold values from -48 to 48
- sink_len: int32 [1], replicated, may hold values from 32 to 128
- window_len: int32 [1], replicated, may hold values from 129 to 640
- block_codes: int32 [16, 5], replicated, may hold values from 0 to 2, as said below
Outputs:
- query_grad: float32 [2048, 8, 128], P(('inner', 'outer'), 'head')
- key_grad: float32 [2048, 128], P(('inner', 'outer'), 'head')
- value_grad: float32 [2048, 128], P(('inner', 'outer'), 'head')
Inputs may be any that keep to these rules, and one draw needn't show every extreme that they name: block_codes[b, 0] is 1 or 2 for every block b.
All inputs are finite; a program needn't handle non-finite values.
Results may differ from a plain program's by a relative error of at most 0.0003.
Values sent between devices are 32-bit elements; how exact they have to be, the bound alone decides.
A program may use at most 64 MiB of HBM per device.

v0:
```python
import math
import jax
import jax.numpy as jnp
from jax import lax
from jax.sharding import PartitionSpec as P

STEPS = 5
SINK = 128
very_low = -1e30
precise = lax.Precision.HIGHEST


def swapped(array, axis, distance):
    return lax.ppermute(array, axis, [(i, i ^ 1 << distance) for i in range(lax.axis_size(axis))])


def spread(array, axis, root):
    mine = lax.axis_index(axis) == root
    return lax.psum(jnp.where(mine, array, jnp.zeros_like(array)), axis)


def shifted(value, axis, steps):
    count = lax.axis_size(axis)
    pairs = [(source, (source + steps) % count) for source in range(count)]
    return lax.ppermute(value, axis, pairs)


def codes_for(block_codes, query_block, offset):
    row_ids = jnp.arange(block_codes.shape[0], dtype=jnp.int32)
    return jnp.sum(jnp.where(row_ids == query_block, block_codes[:, offset], 0))


def visible(query_block, key_block, offset, block_rows, sink_end, window, block_codes, present):
    local_ids = jnp.arange(block_rows, dtype=jnp.int32)
    pos_q = query_block * block_rows + local_ids
    pos_k = key_block * block_rows + local_ids
    code = codes_for(block_codes, query_block, offset)
    near = pos_q[:, None] - pos_k[None, :] < window
    rule = (code != 0) & ((code == 2) | near)
    in_sink = (pos_k < sink_end)[None, :]
    chosen = jnp.where(query_block == 0, in_sink | rule, jnp.logical_not(in_sink) & rule)
    return present & (pos_k[None, :] <= pos_q[:, None]) & chosen


def scores(query_blk, key_blk, temper):
    return temper * jnp.einsum("qhd,kd->hqk", query_blk, key_blk, precision=precise)


def forward_step(running, query_blk, key_blk, value_blk, allowed, temper):
    row_max, row_sum, carried = running
    logits = jnp.where(allowed[None], scores(query_blk, key_blk, temper), very_low)
    new_max = jnp.maximum(row_max, jnp.max(logits, axis=2))
    factor = jnp.exp(row_max - new_max)
    weights = jnp.where(allowed[None], jnp.exp(logits - new_max[:, :, None]), 0.0)
    row_sum = row_sum * factor + jnp.sum(weights, axis=2)
    carried = carried * factor[:, :, None] + jnp.einsum(
        "hqk,kd->hqd", weights, value_blk, precision=precise
    )
    return ((new_max, row_sum, carried), logits)


def finish(running, grad_blk):
    row_max, row_sum, carried = running
    log_sum = row_max + jnp.log(row_sum)
    row_delta = jnp.sum(jnp.transpose(grad_blk, (1, 0, 2)) * carried, axis=2) / row_sum
    return (log_sum, row_delta)


def backward_step(
    query_blk, grad_blk, log_sum, row_delta, key_blk, value_blk, allowed, temper, cached
):
    if cached is None:
        cached = scores(query_blk, key_blk, temper)
    weights = jnp.where(allowed[None], jnp.exp(cached - log_sum[:, :, None]), 0.0)
    grad_dots = jnp.einsum("qhd,kd->hqk", grad_blk, value_blk, precision=precise)
    dscores = weights * (grad_dots - row_delta[:, :, None])
    step_dq = temper * jnp.einsum("hqk,kd->qhd", dscores, key_blk, precision=precise)
    step_dk = temper * jnp.einsum("hqk,qhd->kd", dscores, query_blk, precision=precise)
    step_dv = jnp.einsum("hqk,qhd->kd", weights, grad_blk, precision=precise)
    return (step_dq, step_dk, step_dv)


def shards(queries, key_rows, values, out_grad, sink_len, window_len, block_codes):
    block_rows, heads_dev, head_dim = queries.shape
    temper = 1.0 / math.sqrt(head_dim)
    sink_end = sink_len[0]
    window = window_len[0]
    seq_index = lax.axis_index(("inner", "outer"))
    seq_count = lax.axis_size(("inner", "outer"))
    upper_half = lax.axis_index("head") % 2 == 1
    other_keys, other_values = swapped((key_rows, values), "head", 0)
    key_full = jnp.where(
        upper_half,
        jnp.concatenate([other_keys, key_rows], 1),
        jnp.concatenate([key_rows, other_keys], 1),
    )
    value_full = jnp.where(
        upper_half,
        jnp.concatenate([other_values, values], 1),
        jnp.concatenate([values, other_values], 1),
    )
    sink_keys, sink_values = (
        spread(key_full, ("inner", "outer"), 0),
        spread(value_full, ("inner", "outer"), 0),
    )
    sink_ids = jnp.arange(SINK, dtype=jnp.int32)
    sink_allowed = jnp.broadcast_to(
        ((seq_index >= 1) & (sink_ids < sink_end))[None, :], (block_rows, SINK)
    )
    carried = jnp.zeros((heads_dev, block_rows, head_dim), jnp.float32)
    running = (
        jnp.full((heads_dev, block_rows), very_low, jnp.float32),
        jnp.zeros((heads_dev, block_rows), jnp.float32),
        carried,
    )
    running, ignored = forward_step(running, queries, sink_keys, sink_values, sink_allowed, temper)
    grad_keys = jnp.zeros((block_rows, head_dim), jnp.float32)
    grad_values = jnp.zeros((block_rows, head_dim), jnp.float32)
    moving_k, moving_v = (key_full, value_full)
    cached = None
    for offset in range(STEPS):
        if offset > 0:
            moving_k, moving_v = shifted((moving_k, moving_v), ("inner", "outer"), 1)
        allowed = visible(
            seq_index,
            (seq_index - offset) % seq_count,
            offset,
            block_rows,
            sink_end,
            window,
            block_codes,
            seq_index - offset >= 0,
        )
        running, cached = forward_step(running, queries, moving_k, moving_v, allowed, temper)
    log_sum, row_delta = finish(running, out_grad)
    grad_q = jnp.zeros_like(queries)
    for offset in range(STEPS - 1, -1, -1):
        if offset < STEPS - 1:
            moving_k, moving_v, grad_keys, grad_values = shifted(
                (moving_k, moving_v, grad_keys, grad_values), ("inner", "outer"), -1
            )
            cached = None
        allowed = visible(
            seq_index,
            (seq_index - offset) % seq_count,
            offset,
            block_rows,
            sink_end,
            window,
            block_codes,
            seq_index - offset >= 0,
        )
        step_dq, step_dk, step_dv = backward_step(
            queries, out_grad, log_sum, row_delta, moving_k, moving_v, allowed, temper, cached
        )
        grad_q = grad_q + step_dq
        grad_keys = grad_keys + step_dk
        grad_values = grad_values + step_dv
    sink_dq, sink_dk, sink_dv = backward_step(
        queries, out_grad, log_sum, row_delta, sink_keys, sink_values, sink_allowed, temper, None
    )
    grad_q = grad_q + sink_dq
    total_dk, total_dv = lax.psum((sink_dk, sink_dv), ("inner", "outer"))
    is_first = seq_index == 0
    grad_keys = grad_keys.at[:SINK].add(jnp.where(is_first, total_dk, 0.0))
    grad_values = grad_values.at[:SINK].add(jnp.where(is_first, total_dv, 0.0))
    half_cols = key_rows.shape[1]
    keep_k = jnp.where(upper_half, grad_keys[:, half_cols:], grad_keys[:, :half_cols])
    send_k = jnp.where(upper_half, grad_keys[:, :half_cols], grad_keys[:, half_cols:])
    keep_v = jnp.where(upper_half, grad_values[:, half_cols:], grad_values[:, :half_cols])
    send_v = jnp.where(upper_half, grad_values[:, :half_cols], grad_values[:, half_cols:])
    got_k, got_v = swapped((send_k, send_v), "head", 0)
    return (grad_q, keep_k + got_k, keep_v + got_v)


def solution(mesh):
    in_specs = (
        P(("inner", "outer"), "head", None),
        P(("inner", "outer"), "head"),
        P(("inner", "outer"), "head"),
        P(("inner", "outer"), "head", None),
        P(),
        P(),
        P(),
    )
    out_specs = (
        P(("inner", "outer"), "head", None),
        P(("inner", "outer"), "head"),
        P(("inner", "outer"), "head"),
    )
    return jax.shard_map(shards, mesh=mesh, in_specs=in_specs, out_specs=out_specs, check_vma=False)
```

profile of v0, /device:TPU:8, one launch (start us, length us, event | category | flops | bytes accessed | tf_op | source)
XLA Modules:
  0.0 250.2 jit_solution(6072486249846511252)
XLA Ops:
  7.2 0.9 copy.10
  8.1 1.6 collective-permute-start
  20.8 0.7 broadcast_select_fusion.1
  21.6 1.6 collective-permute-start.1
  23.9 1.6 collective-permute-start.6
  26.2 1.6 collective-permute-start.2
  28.2 88.4 %all-reduce.7.cloned.1.call-done = (f32[128,128]{1,0:T(8,128)}, f32[128,128]{1,0:T(8,128)}) async-done(((f32[128,128]{1,0:T(8,128)}, f32[128,128]{1,0:T(8,128)}), (f32[128,128]{1,0:T(8,128)}, f32[128,128]{1,0:T(8,128)})) %all-reduce.7.cloned.1.call-update) | async-done | bytes 131088 | tf_op jit(solution)/shard_map/psum | solution.py:19
  116.6 1.2 select_reduce_fusion
  117.9 2.0 collective-permute-start.3
  120.3 1.8 collective-permute-done.7
  122.9 1.3 collective-permute-start.4
  124.6 1.8 collective-permute-done.8
  126.4 0.7 collective-permute-start.9
  127.2 1.4 collective-permute-done.4
  132.7 1.1 convolution_bitcast_fusion.6
  134.6 1.0 fusion.49
  136.0 4.2 %collective-permute-start.23 = (f32[128,128]{1,0:T(8,128)S(1)}, f32[128,128]{1,0:T(8,128)S(1)}, u32[]{:S(2)}, u32[]{:S(2)}) collective-permute-start(f32[128,128]{1,0:T(8,128)S(1)} %convolution_bitcast_fusion.11), channel_id=1, source_target_pairs={{0,15},{1,0},{2,1},{3,2},{4,3},{5,4},{6,5},{7,6},{8,7},{9,8},{10,9... | collective-permute-start | bytes 196616 | tf_op jit(solution)/shard_map/ppermute | solution.py:25
  141.0 1.1 collective-permute-start.18
  142.7 3.8 %collective-permute-done.10 = f32[128,128]{1,0:T(8,128)S(1)} collective-permute-done((f32[128,128]{1,0:T(8,128)S(1)}, f32[128,128]{1,0:T(8,128)S(1)}, u32[]{:S(2)}, u32[]{:S(2)}) %collective-permute-start.10) | collective-permute-done | bytes 65568 | tf_op jit(solution)/shard_map/ppermute | solution.py:25
  147.3 1.3 collective-permute-start.24
  149.4 2.3 collective-permute-start.19
  152.3 4.2 %collective-permute-done.12 = f32[128,128]{1,0:T(8,128)S(1)} collective-permute-done((f32[128,128]{1,0:T(8,128)S(1)}, f32[128,128]{1,0:T(8,128)S(1)}, u32[]{:S(2)}, u32[]{:S(2)}) %collective-permute-start.12) | collective-permute-done | bytes 65568 | tf_op jit(solution)/shard_map/ppermute | solution.py:25
  157.3 1.8 collective-permute-start.25
  159.9 1.9 collective-permute-start.20
  162.9 3.8 %collective-permute-done.14 = f32[128,128]{1,0:T(8,128)S(1)} collective-permute-done((f32[128,128]{1,0:T(8,128)S(1)}, f32[128,128]{1,0:T(8,128)S(1)}, u32[]{:S(2)}, u32[]{:S(2)}) %collective-permute-start.14) | collective-permute-done | bytes 65568 | tf_op jit(solution)/shard_map/ppermute | solution.py:25
  167.6 1.7 collective-permute-start.26
  170.1 2.8 %collective-permute-start.21 = (f32[128,128]{1,0:T(8,128)S(1)}, f32[128,128]{1,0:T(8,128)S(1)}, u32[]{:S(2)}, u32[]{:S(2)}) collective-permute-start(f32[128,128]{1,0:T(8,128)S(1)} %add.352), channel_id=1, source_target_pairs={{0,15},{1,0},{2,1},{3,2},{4,3},{5,4},{6,5},{7,6},{8,7},{9,8},{10,9... | collective-permute-start | bytes 196616 | tf_op jit(solution)/shard_map/ppermute | solution.py:25
  173.6 3.6 %collective-permute-done.16 = f32[128,128]{1,0:T(8,128)S(1)} collective-permute-done((f32[128,128]{1,0:T(8,128)S(1)}, f32[128,128]{1,0:T(8,128)S(1)}, u32[]{:S(2)}, u32[]{:S(2)}) %collective-permute-start.16) | collective-permute-done | bytes 65568 | tf_op jit(solution)/shard_map/ppermute | solution.py:25
  177.9 57.4 %all-reduce.5.cloned.1.call-done = (f32[128,128]{1,0:T(8,128)}, f32[128,128]{1,0:T(8,128)}) async-done(((f32[128,128]{1,0:T(8,128)}, f32[128,128]{1,0:T(8,128)}), (f32[128,128]{1,0:T(8,128)}, f32[128,128]{1,0:T(8,128)})) %all-reduce.5.cloned.1.call-update) | async-done | bytes 131088 | tf_op jit(solution)/shard_map/psum | solution.py:163
  235.4 1.5 collective-permute-start.27
  239.4 0.8 copy.78
  241.0 1.6 collective-permute-done.22
  (128 shorter events, 25.2 us)
Async XLA Ops:
  7.2 18.3 %copy-start = (f32[128,4,128]{2,1,0:T(4,128)S(1)}, f32[128,4,128]{2,1,0:T(4,128)}, u32[]{:S(2)}) copy-start(f32[128,4,128]{2,1,0:T(4,128)} %param.15) | copy-start | bytes 786436
  7.2 109.4 %all-reduce.7.cloned.1.call-start = ((), (), s32[]{:S(2)}) async-start(), calls=%async_computation.1 | async-start | bytes 262144 | tf_op jit(solution)/shard_map/psum | solution.py:19
  8.1 12.7 %collective-permute-start = (f32[128,64]{1,0:T(8,128)S(1)}, f32[128,64]{1,0:T(8,128)S(1)}, u32[]{:S(2)}, u32[]{:S(2)}) collective-permute-start(f32[128,64]{1,0:T(8,128)S(1)} %copy.10), channel_id=1, source_target_pairs={{0,16},{16,0},{1,17},{17,1},{2,18},{18,2},{3,19},{19,3},{4,20},{20... | collective-permute-start | bytes 98312 | tf_op jit(solution)/shard_map/ppermute | solution.py:14
  9.8 13.4 %collective-permute-start.5 = (f32[128,64]{1,0:T(8,128)S(1)}, f32[128,64]{1,0:T(8,128)S(1)}, u32[]{:S(2)}, u32[]{:S(2)}) collective-permute-start(f32[128,64]{1,0:T(8,128)S(1)} %copy.24), channel_id=1, source_target_pairs={{0,16},{16,0},{1,17},{17,1},{2,18},{18,2},{3,19},{19,3},{4,20},{20... | collective-permute-start | bytes 98312 | tf_op jit(solution)/shard_map/ppermute | solution.py:14
  10.4 10.3 %copy-start.1 = (f32[128,4,128]{2,1,0:T(4,128)S(1)}, f32[128,4,128]{2,1,0:T(4,128)}, u32[]{:S(2)}) copy-start(f32[128,4,128]{2,1,0:T(4,128)} %param.18) | copy-start | bytes 786436
  21.6 4.6 %collective-permute-start.1 = (f32[128,128]{1,0:T(8,128)S(1)}, f32[128,128]{1,0:T(8,128)S(1)}, u32[]{:S(2)}, u32[]{:S(2)}) collective-permute-start(f32[128,128]{1,0:T(8,128)S(1)} %get-tuple-element.80), channel_id=1, source_target_pairs={{0,1},{1,2},{2,3},{3,4},{4,5},{5,6},{6,7},{7,8},{8,9},{9,10},{10,1... | collective-permute-start | bytes 196616 | tf_op jit(solution)/shard_map/ppermute | solution.py:25
  23.9 94.0 %collective-permute-start.6 = (f32[128,128]{1,0:T(8,128)S(1)}, f32[128,128]{1,0:T(8,128)S(1)}, u32[]{:S(2)}, u32[]{:S(2)}) collective-permute-start(f32[128,128]{1,0:T(8,128)S(1)} %get-tuple-element.78), channel_id=1, source_target_pairs={{0,1},{1,2},{2,3},{3,4},{4,5},{5,6},{6,7},{7,8},{8,9},{9,10},{10,1... | collective-permute-start | bytes 196616 | tf_op jit(solution)/shard_map/ppermute | solution.py:25
  25.9 209.4 %all-reduce.5.cloned.1.call-start = ((), (), s32[]{:S(2)}) async-start(), calls=%async_computation | async-start | bytes 262144 | tf_op jit(solution)/shard_map/psum | solution.py:163
  26.2 91.7 %collective-permute-start.2 = (f32[128,128]{1,0:T(8,128)S(1)}, f32[128,128]{1,0:T(8,128)S(1)}, u32[]{:S(2)}, u32[]{:S(2)}) collective-permute-start(f32[128,128]{1,0:T(8,128)S(1)} %collective-permute-done.1), channel_id=1, source_target_pairs={{0,1},{1,2},{2,3},{3,4},{4,5},{5,6},{6,7},{7,8},{8,9},{9,10},{10,1... | collective-permute-start | bytes 196616 | tf_op jit(solution)/shard_map/ppermute | solution.py:25
  117.8 4.3 %collective-permute-start.7 = (f32[128,128]{1,0:T(8,128)S(1)}, f32[128,128]{1,0:T(8,128)S(1)}, u32[]{:S(2)}, u32[]{:S(2)}) collective-permute-start(f32[128,128]{1,0:T(8,128)S(1)} %collective-permute-done.6), channel_id=1, source_target_pairs={{0,1},{1,2},{2,3},{3,4},{4,5},{5,6},{6,7},{7,8},{8,9},{9,10},{10,1... | collective-permute-start | bytes 196616 | tf_op jit(solution)/shard_map/ppermute | solution.py:25
  117.9 4.9 %collective-permute-start.3 = (f32[128,128]{1,0:T(8,128)S(1)}, f32[128,128]{1,0:T(8,128)S(1)}, u32[]{:S(2)}, u32[]{:S(2)}) collective-permute-start(f32[128,128]{1,0:T(8,128)S(1)} %collective-permute-done.2), channel_id=1, source_target_pairs={{0,1},{1,2},{2,3},{3,4},{4,5},{5,6},{6,7},{7,8},{8,9},{9,10},{10,1... | collective-permute-start | bytes 196616 | tf_op jit(solution)/shard_map/ppermute | solution.py:25
  122.2 4.3 %collective-permute-start.8 = (f32[128,128]{1,0:T(8,128)S(1)}, f32[128,128]{1,0:T(8,128)S(1)}, u32[]{:S(2)}, u32[]{:S(2)}) collective-permute-start(f32[128,128]{1,0:T(8,128)S(1)} %collective-permute-done.7), channel_id=1, source_target_pairs={{0,1},{1,2},{2,3},{3,4},{4,5},{5,6},{6,7},{7,8},{8,9},{9,10},{10,1... | collective-permute-start | bytes 196616 | tf_op jit(solution)/shard_map/ppermute | solution.py:25
  122.9 5.7 %collective-permute-start.4 = (f32[128,128]{1,0:T(8,128)S(1)}, f32[128,128]{1,0:T(8,128)S(1)}, u32[]{:S(2)}, u32[]{:S(2)}) collective-permute-start(f32[128,128]{1,0:T(8,128)S(1)} %collective-permute-done.3), channel_id=1, source_target_pairs={{0,1},{1,2},{2,3},{3,4},{4,5},{5,6},{6,7},{7,8},{8,9},{9,10},{10,1... | collective-permute-start | bytes 196616 | tf_op jit(solution)/shard_map/ppermute | solution.py:25
  126.4 7.3 %collective-permute-start.9 = (f32[128,128]{1,0:T(8,128)S(1)}, f32[128,128]{1,0:T(8,128)S(1)}, u32[]{:S(2)}, u32[]{:S(2)}) collective-permute-start(f32[128,128]{1,0:T(8,128)S(1)} %collective-permute-done.8), channel_id=1, source_target_pairs={{0,1},{1,2},{2,3},{3,4},{4,5},{5,6},{6,7},{7,8},{8,9},{9,10},{10,1... | collective-permute-start | bytes 196616 | tf_op jit(solution)/shard_map/ppermute | solution.py:25
  136.0 10.9 %collective-permute-start.23 = (f32[128,128]{1,0:T(8,128)S(1)}, f32[128,128]{1,0:T(8,128)S(1)}, u32[]{:S(2)}, u32[]{:S(2)}) collective-permute-start(f32[128,128]{1,0:T(8,128)S(1)} %convolution_bitcast_fusion.11), channel_id=1, source_target_pairs={{0,15},{1,0},{2,1},{3,2},{4,3},{5,4},{6,5},{7,6},{8,7},{9,8},{10,9... | collective-permute-start | bytes 196616 | tf_op jit(solution)/shard_map/ppermute | solution.py:25
  141.0 8.0 %collective-permute-start.18 = (f32[128,128]{1,0:T(8,128)S(1)}, f32[128,128]{1,0:T(8,128)S(1)}, u32[]{:S(2)}, u32[]{:S(2)}) collective-permute-start(f32[128,128]{1,0:T(8,128)S(1)} %fusion.54), channel_id=1, source_target_pairs={{0,15},{1,0},{2,1},{3,2},{4,3},{5,4},{6,5},{7,6},{8,7},{9,8},{10,9... | collective-permute-start | bytes 196616 | tf_op jit(solution)/shard_map/ppermute | solution.py:25
  142.2 4.3 %collective-permute-start.10 = (f32[128,128]{1,0:T(8,128)S(1)}, f32[128,128]{1,0:T(8,128)S(1)}, u32[]{:S(2)}, u32[]{:S(2)}) collective-permute-start(f32[128,128]{1,0:T(8,128)S(1)} %collective-permute-done.4), channel_id=1, source_target_pairs={{0,15},{1,0},{2,1},{3,2},{4,3},{5,4},{6,5},{7,6},{8,7},{9,8},{10,9... | collective-permute-start | bytes 196616 | tf_op jit(solution)/shard_map/ppermute | solution.py:25
  142.2 6.4 %collective-permute-start.11 = (f32[128,128]{1,0:T(8,128)S(1)}, f32[128,128]{1,0:T(8,128)S(1)}, u32[]{:S(2)}, u32[]{:S(2)}) collective-permute-start(f32[128,128]{1,0:T(8,128)S(1)} %collective-permute-done.9), channel_id=1, source_target_pairs={{0,15},{1,0},{2,1},{3,2},{4,3},{5,4},{6,5},{7,6},{8,7},{9,8},{10,9... | collective-permute-start | bytes 196616 | tf_op jit(solution)/shard_map/ppermute | solution.py:25
  147.3 10.0 %collective-permute-start.24 = (f32[128,128]{1,0:T(8,128)S(1)}, f32[128,128]{1,0:T(8,128)S(1)}, u32[]{:S(2)}, u32[]{:S(2)}) collective-permute-start(f32[128,128]{1,0:T(8,128)S(1)} %fusion.56), channel_id=1, source_target_pairs={{0,15},{1,0},{2,1},{3,2},{4,3},{5,4},{6,5},{7,6},{8,7},{9,8},{10,9... | collective-permute-start | bytes 196616 | tf_op jit(solution)/shard_map/ppermute | solution.py:25
  149.4 10.5 %collective-permute-start.19 = (f32[128,128]{1,0:T(8,128)S(1)}, f32[128,128]{1,0:T(8,128)S(1)}, u32[]{:S(2)}, u32[]{:S(2)}) collective-permute-start(f32[128,128]{1,0:T(8,128)S(1)} %fusion.55), channel_id=1, source_target_pairs={{0,15},{1,0},{2,1},{3,2},{4,3},{5,4},{6,5},{7,6},{8,7},{9,8},{10,9... | collective-permute-start | bytes 196616 | tf_op jit(solution)/shard_map/ppermute | solution.py:25
  151.7 4.8 %collective-permute-start.12 = (f32[128,128]{1,0:T(8,128)S(1)}, f32[128,128]{1,0:T(8,128)S(1)}, u32[]{:S(2)}, u32[]{:S(2)}) collective-permute-start(f32[128,128]{1,0:T(8,128)S(1)} %collective-permute-done.10), channel_id=1, source_target_pairs={{0,15},{1,0},{2,1},{3,2},{4,3},{5,4},{6,5},{7,6},{8,7},{9,8},{10,9... | collective-permute-start | bytes 196616 | tf_op jit(solution)/shard_map/ppermute | solution.py:25
  151.8 7.4 %collective-permute-start.13 = (f32[128,128]{1,0:T(8,128)S(1)}, f32[128,128]{1,0:T(8,128)S(1)}, u32[]{:S(2)}, u32[]{:S(2)}) collective-permute-start(f32[128,128]{1,0:T(8,128)S(1)} %collective-permute-done.11), channel_id=1, source_target_pairs={{0,15},{1,0},{2,1},{3,2},{4,3},{5,4},{6,5},{7,6},{8,7},{9,8},{10,9... | collective-permute-start | bytes 196616 | tf_op jit(solution)/shard_map/ppermute | solution.py:25
  157.3 10.2 %collective-permute-start.25 = (f32[128,128]{1,0:T(8,128)S(1)}, f32[128,128]{1,0:T(8,128)S(1)}, u32[]{:S(2)}, u32[]{:S(2)}) collective-permute-start(f32[128,128]{1,0:T(8,128)S(1)} %add.357), channel_id=1, source_target_pairs={{0,15},{1,0},{2,1},{3,2},{4,3},{5,4},{6,5},{7,6},{8,7},{9,8},{10,9... | collective-permute-start | bytes 196616 | tf_op jit(solution)/shard_map/ppermute | solution.py:25
  159.9 10.1 %collective-permute-start.20 = (f32[128,128]{1,0:T(8,128)S(1)}, f32[128,128]{1,0:T(8,128)S(1)}, u32[]{:S(2)}, u32[]{:S(2)}) collective-permute-start(f32[128,128]{1,0:T(8,128)S(1)} %add.351), channel_id=1, source_target_pairs={{0,15},{1,0},{2,1},{3,2},{4,3},{5,4},{6,5},{7,6},{8,7},{9,8},{10,9... | collective-permute-start | bytes 196616 | tf_op jit(solution)/shard_map/ppermute | solution.py:25
  161.9 4.9 %collective-permute-start.14 = (f32[128,128]{1,0:T(8,128)S(1)}, f32[128,128]{1,0:T(8,128)S(1)}, u32[]{:S(2)}, u32[]{:S(2)}) collective-permute-start(f32[128,128]{1,0:T(8,128)S(1)} %collective-permute-done.12), channel_id=1, source_target_pairs={{0,15},{1,0},{2,1},{3,2},{4,3},{5,4},{6,5},{7,6},{8,7},{9,8},{10,9... | collective-permute-start | bytes 196616 | tf_op jit(solution)/shard_map/ppermute | solution.py:25
  162.4 6.8 %collective-permute-start.15 = (f32[128,128]{1,0:T(8,128)S(1)}, f32[128,128]{1,0:T(8,128)S(1)}, u32[]{:S(2)}, u32[]{:S(2)}) collective-permute-start(f32[128,128]{1,0:T(8,128)S(1)} %collective-permute-done.13), channel_id=1, source_target_pairs={{0,15},{1,0},{2,1},{3,2},{4,3},{5,4},{6,5},{7,6},{8,7},{9,8},{10,9... | collective-permute-start | bytes 196616 | tf_op jit(solution)/shard_map/ppermute | solution.py:25
  167.6 67.7 %collective-permute-start.26 = (f32[128,128]{1,0:T(8,128)S(1)}, f32[128,128]{1,0:T(8,128)S(1)}, u32[]{:S(2)}, u32[]{:S(2)}) collective-permute-start(f32[128,128]{1,0:T(8,128)S(1)} %add.358), channel_id=1, source_target_pairs={{0,15},{1,0},{2,1},{3,2},{4,3},{5,4},{6,5},{7,6},{8,7},{9,8},{10,9... | collective-permute-start | bytes 196616 | tf_op jit(solution)/shard_map/ppermute | solution.py:25
  170.1 67.7 %collective-permute-start.21 = (f32[128,128]{1,0:T(8,128)S(1)}, f32[128,128]{1,0:T(8,128)S(1)}, u32[]{:S(2)}, u32[]{:S(2)}) collective-permute-start(f32[128,128]{1,0:T(8,128)S(1)} %add.352), channel_id=1, source_target_pairs={{0,15},{1,0},{2,1},{3,2},{4,3},{5,4},{6,5},{7,6},{8,7},{9,8},{10,9... | collective-permute-start | bytes 196616 | tf_op jit(solution)/shard_map/ppermute | solution.py:25
  172.9 4.3 %collective-permute-start.16 = (f32[128,128]{1,0:T(8,128)S(1)}, f32[128,128]{1,0:T(8,128)S(1)}, u32[]{:S(2)}, u32[]{:S(2)}) collective-permute-start(f32[128,128]{1,0:T(8,128)S(1)} %collective-permute-done.14), channel_id=1, source_target_pairs={{0,15},{1,0},{2,1},{3,2},{4,3},{5,4},{6,5},{7,6},{8,7},{9,8},{10,9... | collective-permute-start | bytes 196616 | tf_op jit(solution)/shard_map/ppermute | solution.py:25
  173.1 63.9 %collective-permute-start.17 = (f32[128,128]{1,0:T(8,128)S(1)}, f32[128,128]{1,0:T(8,128)S(1)}, u32[]{:S(2)}, u32[]{:S(2)}) collective-permute-start(f32[128,128]{1,0:T(8,128)S(1)} %collective-permute-done.15), channel_id=1, source_target_pairs={{0,15},{1,0},{2,1},{3,2},{4,3},{5,4},{6,5},{7,6},{8,7},{9,8},{10,9... | collective-permute-start | bytes 196616 | tf_op jit(solution)/shard_map/ppermute | solution.py:25
  235.4 4.8 %collective-permute-start.27 = (f32[128,64]{1,0:T(8,128)S(1)}, f32[128,64]{1,0:T(8,128)S(1)}, u32[]{:S(2)}, u32[]{:S(2)}) collective-permute-start(f32[128,64]{1,0:T(8,128)S(1)} %slice_select_fusion), channel_id=1, source_target_pairs={{0,16},{16,0},{1,17},{17,1},{2,18},{18,2},{3,19},{19,3},{4,20},{20... | collective-permute-start | bytes 98312 | tf_op jit(solution)/shard_map/ppermute | solution.py:14
  238.3 4.3 %collective-permute-start.22 = (f32[128,64]{1,0:T(8,128)S(1)}, f32[128,64]{1,0:T(8,128)S(1)}, u32[]{:S(2)}, u32[]{:S(2)}) collective-permute-start(f32[128,64]{1,0:T(8,128)S(1)} %slice_select_fusion.1), channel_id=1, source_target_pairs={{0,16},{16,0},{1,17},{17,1},{2,18},{18,2},{3,19},{19,3},{4,20},{20... | collective-permute-start | bytes 98312 | tf_op jit(solution)/shard_map/ppermute | solution.py:14
  (5 other events, 5.9 us)
Sparse Core Ops, SparseCore 0:
  26.0 90.5 all-reduce.6
  142.3 92.9 all-reduce.4
where the time goes:
time: 251 us; the launch traced here: 250 us
  waiting for transfers between devices  169 us (67%)
  starting transfers between devices  31.6 us (13%)
  between operations  22.4 us (9%)
  matrix products  18.4 us (7%)
  local copies, waits for them, and re-layouts  5.47 us (2%)
  other arithmetic  3.54 us (1%)
    psum x1, waiting for transfers between devices, spread(): return lax.psum(jnp.where(mine, array, jnp.zeros_like(array)), axis)  88.4 us
    psum x1, waiting for transfers between devices, shards(): total_dk, total_dv = lax.psum((sink_dk, sink_dv), ('inner', 'outer'))  57.4 us
    ppermute x24, starting transfers between devices, shifted(): return lax.ppermute(value, axis, pairs)  27.2 us
    ppermute x24, waiting for transfers between devices, shifted(): return lax.ppermute(value, axis, pairs)  21.4 us
  transfers between devices with their start and end apart: 30, of which 12 were waited for; matrix products, arithmetic and copies ran while one was open for 9% of the time, Pallas kernels for 0%

commit v1 on v0

--- a/solution.py
+++ b/solution.py
@@ -16,7 +16,7 @@
 
 def spread(array, axis, root):
     mine = lax.axis_index(axis) == root
-    return lax.psum(jnp.where(mine, array, jnp.zeros_like(array)), axis)
+    return jnp.sum(lax.all_gather(jnp.where(mine, array, jnp.zeros_like(array)), axis), axis=0)
 
 
 def shifted(value, axis, steps):

time: 251 us -> 218 us (0.87)
  waiting for transfers between devices: 169 us -> 108 us
  starting transfers between devices: 31.6 us -> 51.1 us
  matrix products: 18.4 us -> 22.2 us
  other arithmetic: 3.54 us -> 6.33 us
    psum x1 -> x0, waiting for transfers between devices: 88.4 us -> none  [spread(): return lax.psum(jnp.where(mine, array, jnp.zeros_like(array)), axis)]
    ppermute x24, starting transfers between devices: 27.2 us -> 46.5 us  [shifted(): return lax.ppermute(value, axis, pairs)]
    all_gather x0 -> x2, waiting for transfers between devices: none -> 18.6 us  [spread(): lax.all_gather(jnp.where(mine, array, jnp.zeros_like(array)), axis)]
    psum x1, waiting for transfers between devices: 57.4 us -> 69.1 us  [shards(): total_dk, total_dv = lax.psum((sink_dk, sink_dv), ('inner', 'outer'))]
    ppermute x24, waiting for transfers between devices: 21.4 us -> 15.3 us  [shifted(): return lax.ppermute(value, axis, pairs)]
    ppermute x4, waiting for transfers between devices: 1.64 us -> 5.35 us  [swapped(): lax.ppermute(array, axis, [(i, i ^ 1 << distance) for i in range(lax.axis...]
    reduce_sum x0 -> x2, other arithmetic: none -> 2.57 us  [spread(): jnp.sum(lax.all_gather(jnp.where(mine, array, jnp.zeros_like(array)), axi...]
    unnamed x20 -> x38, local copies, waits for them, and re-layouts: 4.87 us -> 6.15 us
  transfers between devices with their start and end apart: 30 -> 31, of which waited for: 12 -> 14; matrix products, arithmetic and copies ran while one was open for 9% -> 14% of each run, Pallas kernels for 0% -> 0%
where the time goes in v1:
time: 218 us; the launch traced here: 217 us
  waiting for transfers between devices  108 us (50%)
  starting transfers between devices  51.1 us (23%)
  matrix products  22.2 us (10%)
  between operations  22 us (10%)
  local copies, waits for them, and re-layouts  6.76 us (3%)
  other arithmetic  6.33 us (3%)
    psum x1, waiting for transfers between devices, shards(): total_dk, total_dv = lax.psum((sink_dk, sink_dv), ('inner', 'outer'))  69.1 us
    ppermute x24, starting transfers between devices, shifted(): return lax.ppermute(value, axis, pairs)  46.5 us
    all_gather x2, waiting for transfers between devices, spread(): lax.all_gather(jnp.where(mine, array, jnp.zeros_like(array)), axis)  18.6 us
    ppermute x24, waiting for transfers between devices, shifted(): return lax.ppermute(value, axis, pairs)  15.3 us
    unnamed x38, local copies, waits for them, and re-layouts  6.15 us
    ppermute x4, waiting for transfers between devices, swapped(): lax.ppermute(array, axis, [(i, i ^ 1 << distance) for i in range(lax.axis...  5.35 us
    dot_general x6, matrix products, backward_step(): step_dv = jnp.einsum('hqk,qhd->kd', weights, grad_blk, precision=precise)  4.51 us
    dot_general x6, matrix products, backward_step(): jnp.einsum('hqk,qhd->kd', dscores, query_blk, precision=precise)  4.44 us
  transfers between devices with their start and end apart: 31, of which 14 were waited for; matrix products, arithmetic and copies ran while one was open for 14% of the time, Pallas kernels for 0%

profile of v1, /device:TPU:8, one launch (start us, length us, event | category | flops | bytes accessed | tf_op | source)
XLA Modules:
  0.0 216.8 jit_solution(17355548724396531470)
XLA Ops:
  8.1 1.6 collective-permute-start
  10.4 2.5 %collective-permute-done = f32[128,64]{1,0:T(8,128)S(1)} collective-permute-done((f32[128,64]{1,0:T(8,128)S(1)}, f32[128,64]{1,0:T(8,128)S(1)}, u32[]{:S(2)}, u32[]{:S(2)}) %collective-permute-start) | collective-permute-done | bytes 32800 | tf_op jit(solution)/shard_map/ppermute | solution.py:14
  24.1 1.6 collective-permute-start.6
  25.8 1.6 collective-permute-start.1
  27.5 1.3 collective-permute-done.6
  28.8 1.6 collective-permute-start.7
  30.4 2.4 %collective-permute-start.2 = (f32[128,128]{1,0:T(8,128)S(1)}, f32[128,128]{1,0:T(8,128)S(1)}, u32[]{:S(2)}, u32[]{:S(2)}) collective-permute-start(f32[128,128]{1,0:T(8,128)S(1)} %collective-permute-done.1), channel_id=1, source_target_pairs={{0,1},{1,2},{2,3},{3,4},{4,5},{5,6},{6,7},{7,8},{8,9},{9,10},{10,1... | collective-permute-start | bytes 196616 | tf_op jit(solution)/shard_map/ppermute | solution.py:25
  33.6 1.7 collective-permute-start.8
  35.7 1.3 collective-permute-start.3
  37.4 1.8 collective-permute-done.8
  39.5 4.0 %collective-permute-done.3 = f32[128,128]{1,0:T(8,128)S(1)} collective-permute-done((f32[128,128]{1,0:T(8,128)S(1)}, f32[128,128]{1,0:T(8,128)S(1)}, u32[]{:S(2)}, u32[]{:S(2)}) %collective-permute-start.3) | collective-permute-done | bytes 65568 | tf_op jit(solution)/shard_map/ppermute | solution.py:25
  43.9 3.8 %collective-permute-done.9 = f32[128,128]{1,0:T(8,128)S(1)} collective-permute-done((f32[128,128]{1,0:T(8,128)S(1)}, f32[128,128]{1,0:T(8,128)S(1)}, u32[]{:S(2)}, u32[]{:S(2)}) %collective-permute-start.9) | collective-permute-done | bytes 65568 | tf_op jit(solution)/shard_map/ppermute | solution.py:25
  47.7 4.3 %collective-permute-start.11 = (f32[128,128]{1,0:T(8,128)S(1)}, f32[128,128]{1,0:T(8,128)S(1)}, u32[]{:S(2)}, u32[]{:S(2)}) collective-permute-start(f32[128,128]{1,0:T(8,128)S(1)} %collective-permute-done.9), channel_id=1, source_target_pairs={{0,15},{1,0},{2,1},{3,2},{4,3},{5,4},{6,5},{7,6},{8,7},{9,8},{10,9... | collective-permute-start | bytes 196616 | tf_op jit(solution)/shard_map/ppermute | solution.py:25
  52.0 2.1 collective-permute-start.10
  54.6 1.7 collective-permute-start.13
  56.5 2.5 %collective-permute-start.12 = (f32[128,128]{1,0:T(8,128)S(1)}, f32[128,128]{1,0:T(8,128)S(1)}, u32[]{:S(2)}, u32[]{:S(2)}) collective-permute-start(f32[128,128]{1,0:T(8,128)S(1)} %collective-permute-done.10), channel_id=1, source_target_pairs={{0,15},{1,0},{2,1},{3,2},{4,3},{5,4},{6,5},{7,6},{8,7},{9,8},{10,9... | collective-permute-start | bytes 196616 | tf_op jit(solution)/shard_map/ppermute | solution.py:25
  59.4 2.0 collective-permute-start.15
  61.4 3.4 %collective-permute-start.14 = (f32[128,128]{1,0:T(8,128)S(1)}, f32[128,128]{1,0:T(8,128)S(1)}, u32[]{:S(2)}, u32[]{:S(2)}) collective-permute-start(f32[128,128]{1,0:T(8,128)S(1)} %collective-permute-done.12), channel_id=1, source_target_pairs={{0,15},{1,0},{2,1},{3,2},{4,3},{5,4},{6,5},{7,6},{8,7},{9,8},{10,9... | collective-permute-start | bytes 196616 | tf_op jit(solution)/shard_map/ppermute | solution.py:25
  65.2 2.6 %collective-permute-start.17 = (f32[128,128]{1,0:T(8,128)}, f32[128,128]{1,0:T(8,128)}, u32[]{:S(2)}, u32[]{:S(2)}) collective-permute-start(f32[128,128]{1,0:T(8,128)} %collective-permute-done.15), channel_id=1, source_target_pairs={{0,15},{1,0},{2,1},{3,2},{4,3},{5,4},{6,5},{7,6},{8,7},{9,8},{10,9... | collective-permute-start | bytes 196616 | tf_op jit(solution)/shard_map/ppermute | solution.py:25
  67.8 4.5 %collective-permute-start.16 = (f32[128,128]{1,0:T(8,128)S(1)}, f32[128,128]{1,0:T(8,128)S(1)}, u32[]{:S(2)}, u32[]{:S(2)}) collective-permute-start(f32[128,128]{1,0:T(8,128)S(1)} %collective-permute-done.14), channel_id=1, source_target_pairs={{0,15},{1,0},{2,1},{3,2},{4,3},{5,4},{6,5},{7,6},{8,7},{9,8},{10,9... | collective-permute-start | bytes 196616 | tf_op jit(solution)/shard_map/ppermute | solution.py:25
  72.3 1.3 reduce_sum.125
  75.6 18.6 %all-gather.5.cloned.1.call-done = f32[16,128,128]{2,1,0:T(8,128)} async-done(((f32[1,128,128]{2,1,0:T(8,128)}), f32[16,128,128]{2,1,0:T(8,128)}) %all-gather.5.cloned.1.call-update) | async-done | bytes 1048592 | tf_op jit(solution)/shard_map/all_gather | solution.py:19
  94.2 1.3 reduce_sum.158
  100.1 1.6 collective-permute-start.23
  103.1 2.1 collective-permute-start.18
  117.2 1.2 fusion.56
  120.9 2.3 %collective-permute-done.24 = f32[128,128]{1,0:T(8,128)S(1)} collective-permute-done((f32[128,128]{1,0:T(8,128)S(1)}, f32[128,128]{1,0:T(8,128)S(1)}, u32[]{:S(2)}, u32[]{:S(2)}) %collective-permute-start.24) | collective-permute-done | bytes 65568 | tf_op jit(solution)/shard_map/ppermute | solution.py:25
  124.4 2.5 %collective-permute-start.20 = (f32[128,128]{1,0:T(8,128)S(1)}, f32[128,128]{1,0:T(8,128)S(1)}, u32[]{:S(2)}, u32[]{:S(2)}) collective-permute-start(f32[128,128]{1,0:T(8,128)S(1)} %add.347), channel_id=1, source_target_pairs={{0,15},{1,0},{2,1},{3,2},{4,3},{5,4},{6,5},{7,6},{8,7},{9,8},{10,9... | collective-permute-start | bytes 196616 | tf_op jit(solution)/shard_map/ppermute | solution.py:25
  129.7 4.6 %collective-permute-start.21 = (f32[128,128]{1,0:T(8,128)S(1)}, f32[128,128]{1,0:T(8,128)S(1)}, u32[]{:S(2)}, u32[]{:S(2)}) collective-permute-start(f32[128,128]{1,0:T(8,128)S(1)} %add.348), channel_id=1, source_target_pairs={{0,15},{1,0},{2,1},{3,2},{4,3},{5,4},{6,5},{7,6},{8,7},{9,8},{10,9... | collective-permute-start | bytes 196616 | tf_op jit(solution)/shard_map/ppermute | solution.py:25
  134.3 69.1 %all-reduce.3.cloned.1.call-done = (f32[128,128]{1,0:T(8,128)}, f32[128,128]{1,0:T(8,128)}) async-done(((f32[128,128]{1,0:T(8,128)}, f32[128,128]{1,0:T(8,128)}), (f32[128,128]{1,0:T(8,128)}, f32[128,128]{1,0:T(8,128)})) %all-reduce.3.cloned.1.call-update) | async-done | bytes 131088 | tf_op jit(solution)/shard_map/psum | solution.py:163
  203.5 1.5 collective-permute-start.27
  205.9 2.0 collective-permute-done.27
  (153 shorter events, 38.4 us)
Async XLA Ops:
  7.2 65.1 %all-gather.3.cloned.1.call-start = ((), (), s32[]{:S(2)}) async-start(), calls=%async_computation | async-start | bytes 1114112 | tf_op jit(solution)/shard_map/all_gather | solution.py:19
  8.1 4.8 %collective-permute-start = (f32[128,64]{1,0:T(8,128)S(1)}, f32[128,64]{1,0:T(8,128)S(1)}, u32[]{:S(2)}, u32[]{:S(2)}) collective-permute-start(f32[128,64]{1,0:T(8,128)S(1)} %copy.83), channel_id=1, source_target_pairs={{0,16},{16,0},{1,17},{17,1},{2,18},{18,2},{3,19},{19,3},{4,20},{20... | collective-permute-start | bytes 98312 | tf_op jit(solution)/shard_map/ppermute | solution.py:14
  9.8 14.2 %collective-permute-start.5 = (f32[128,64]{1,0:T(8,128)S(1)}, f32[128,64]{1,0:T(8,128)S(1)}, u32[]{:S(2)}, u32[]{:S(2)}) collective-permute-start(f32[128,64]{1,0:T(8,128)S(1)} %copy.98), channel_id=1, source_target_pairs={{0,16},{16,0},{1,17},{17,1},{2,18},{18,2},{3,19},{19,3},{4,20},{20... | collective-permute-start | bytes 98312 | tf_op jit(solution)/shard_map/ppermute | solution.py:14
  13.7 80.5 %all-gather.5.cloned.1.call-start = ((), (), s32[]{:S(2)}) async-start(), calls=%async_computation.1 | async-start | bytes 1114112 | tf_op jit(solution)/shard_map/all_gather | solution.py:19
  24.1 4.7 %collective-permute-start.6 = (f32[128,128]{1,0:T(8,128)S(1)}, f32[128,128]{1,0:T(8,128)S(1)}, u32[]{:S(2)}, u32[]{:S(2)}) collective-permute-start(f32[128,128]{1,0:T(8,128)S(1)} %maximum_select_fusion.2), channel_id=1, source_target_pairs={{0,1},{1,2},{2,3},{3,4},{4,5},{5,6},{6,7},{7,8},{8,9},{9,10},{10,1... | collective-permute-start | bytes 196616 | tf_op jit(solution)/shard_map/ppermute | solution.py:25
  25.8 4.5 %collective-permute-start.1 = (f32[128,128]{1,0:T(8,128)S(1)}, f32[128,128]{1,0:T(8,128)S(1)}, u32[]{:S(2)}, u32[]{:S(2)}) collective-permute-start(f32[128,128]{1,0:T(8,128)S(1)} %maximum_select_fusion), channel_id=1, source_target_pairs={{0,1},{1,2},{2,3},{3,4},{4,5},{5,6},{6,7},{7,8},{8,9},{9,10},{10,1... | collective-permute-start | bytes 196616 | tf_op jit(solution)/shard_map/ppermute | solution.py:25
  28.8 4.8 %collective-permute-start.7 = (f32[128,128]{1,0:T(8,128)S(1)}, f32[128,128]{1,0:T(8,128)S(1)}, u32[]{:S(2)}, u32[]{:S(2)}) collective-permute-start(f32[128,128]{1,0:T(8,128)S(1)} %collective-permute-done.6), channel_id=1, source_target_pairs={{0,1},{1,2},{2,3},{3,4},{4,5},{5,6},{6,7},{7,8},{8,9},{9,10},{10,1... | collective-permute-start | bytes 196616 | tf_op jit(solution)/shard_map/ppermute | solution.py:25
  30.4 5.4 %collective-permute-start.2 = (f32[128,128]{1,0:T(8,128)S(1)}, f32[128,128]{1,0:T(8,128)S(1)}, u32[]{:S(2)}, u32[]{:S(2)}) collective-permute-start(f32[128,128]{1,0:T(8,128)S(1)} %collective-permute-done.1), channel_id=1, source_target_pairs={{0,1},{1,2},{2,3},{3,4},{4,5},{5,6},{6,7},{7,8},{8,9},{9,10},{10,1... | collective-permute-start | bytes 196616 | tf_op jit(solution)/shard_map/ppermute | solution.py:25
  33.5 169.9 %all-reduce.3.cloned.1.call-start = ((), (), s32[]{:S(2)}) async-start(), calls=%async_computation.2 | async-start | bytes 262144 | tf_op jit(solution)/shard_map/psum | solution.py:163
  33.6 5.7 %collective-permute-start.8 = (f32[128,128]{1,0:T(8,128)S(1)}, f32[128,128]{1,0:T(8,128)S(1)}, u32[]{:S(2)}, u32[]{:S(2)}) collective-permute-start(f32[128,128]{1,0:T(8,128)S(1)} %collective-permute-done.7), channel_id=1, source_target_pairs={{0,1},{1,2},{2,3},{3,4},{4,5},{5,6},{6,7},{7,8},{8,9},{9,10},{10,1... | collective-permute-start | bytes 196616 | tf_op jit(solution)/shard_map/ppermute | solution.py:25
  35.7 7.8 %collective-permute-start.3 = (f32[128,128]{1,0:T(8,128)S(1)}, f32[128,128]{1,0:T(8,128)S(1)}, u32[]{:S(2)}, u32[]{:S(2)}) collective-permute-start(f32[128,128]{1,0:T(8,128)S(1)} %collective-permute-done.2), channel_id=1, source_target_pairs={{0,1},{1,2},{2,3},{3,4},{4,5},{5,6},{6,7},{7,8},{8,9},{9,10},{10,1... | collective-permute-start | bytes 196616 | tf_op jit(solution)/shard_map/ppermute | solution.py:25
  39.2 8.5 %collective-permute-start.9 = (f32[128,128]{1,0:T(8,128)S(1)}, f32[128,128]{1,0:T(8,128)S(1)}, u32[]{:S(2)}, u32[]{:S(2)}) collective-permute-start(f32[128,128]{1,0:T(8,128)S(1)} %collective-permute-done.8), channel_id=1, source_target_pairs={{0,1},{1,2},{2,3},{3,4},{4,5},{5,6},{6,7},{7,8},{8,9},{9,10},{10,1... | collective-permute-start | bytes 196616 | tf_op jit(solution)/shard_map/ppermute | solution.py:25
  43.5 8.5 %collective-permute-start.4 = (f32[128,128]{1,0:T(8,128)S(1)}, f32[128,128]{1,0:T(8,128)S(1)}, u32[]{:S(2)}, u32[]{:S(2)}) collective-permute-start(f32[128,128]{1,0:T(8,128)S(1)} %collective-permute-done.3), channel_id=1, source_target_pairs={{0,1},{1,2},{2,3},{3,4},{4,5},{5,6},{6,7},{7,8},{8,9},{9,10},{10,1... | collective-permute-start | bytes 196616 | tf_op jit(solution)/shard_map/ppermute | solution.py:25
  47.7 6.9 %collective-permute-start.11 = (f32[128,128]{1,0:T(8,128)S(1)}, f32[128,128]{1,0:T(8,128)S(1)}, u32[]{:S(2)}, u32[]{:S(2)}) collective-permute-start(f32[128,128]{1,0:T(8,128)S(1)} %collective-permute-done.9), channel_id=1, source_target_pairs={{0,15},{1,0},{2,1},{3,2},{4,3},{5,4},{6,5},{7,6},{8,7},{9,8},{10,9... | collective-permute-start | bytes 196616 | tf_op jit(solution)/shard_map/ppermute | solution.py:25
  52.0 4.5 %collective-permute-start.10 = (f32[128,128]{1,0:T(8,128)S(1)}, f32[128,128]{1,0:T(8,128)S(1)}, u32[]{:S(2)}, u32[]{:S(2)}) collective-permute-start(f32[128,128]{1,0:T(8,128)S(1)} %collective-permute-done.4), channel_id=1, source_target_pairs={{0,15},{1,0},{2,1},{3,2},{4,3},{5,4},{6,5},{7,6},{8,7},{9,8},{10,9... | collective-permute-start | bytes 196616 | tf_op jit(solution)/shard_map/ppermute | solution.py:25
  54.6 4.8 %collective-permute-start.13 = (f32[128,128]{1,0:T(8,128)S(1)}, f32[128,128]{1,0:T(8,128)S(1)}, u32[]{:S(2)}, u32[]{:S(2)}) collective-permute-start(f32[128,128]{1,0:T(8,128)S(1)} %collective-permute-done.11), channel_id=1, source_target_pairs={{0,15},{1,0},{2,1},{3,2},{4,3},{5,4},{6,5},{7,6},{8,7},{9,8},{10,9... | collective-permute-start | bytes 196616 | tf_op jit(solution)/shard_map/ppermute | solution.py:25
  56.5 4.9 %collective-permute-start.12 = (f32[128,128]{1,0:T(8,128)S(1)}, f32[128,128]{1,0:T(8,128)S(1)}, u32[]{:S(2)}, u32[]{:S(2)}) collective-permute-start(f32[128,128]{1,0:T(8,128)S(1)} %collective-permute-done.10), channel_id=1, source_target_pairs={{0,15},{1,0},{2,1},{3,2},{4,3},{5,4},{6,5},{7,6},{8,7},{9,8},{10,9... | collective-permute-start | bytes 196616 | tf_op jit(solution)/shard_map/ppermute | solution.py:25
  59.4 5.8 %collective-permute-start.15 = (f32[128,128]{1,0:T(8,128)S(1)}, f32[128,128]{1,0:T(8,128)}, u32[]{:S(2)}, u32[]{:S(2)}) collective-permute-start(f32[128,128]{1,0:T(8,128)S(1)} %collective-permute-done.13), channel_id=1, source_target_pairs={{0,15},{1,0},{2,1},{3,2},{4,3},{5,4},{6,5},{7,6},{8,7},{9,8},{10,9... | collective-permute-start | bytes 196616 | tf_op jit(solution)/shard_map/ppermute | solution.py:25
  61.4 43.8 %copy-start.2 = (f32[128,128]{1,0:T(8,128)}, f32[128,128]{1,0:T(8,128)S(1)}, u32[]{:S(2)}) copy-start(f32[128,128]{1,0:T(8,128)S(1)} %collective-permute-done.12) | copy-start | bytes 196612
  61.4 6.4 %collective-permute-start.14 = (f32[128,128]{1,0:T(8,128)S(1)}, f32[128,128]{1,0:T(8,128)S(1)}, u32[]{:S(2)}, u32[]{:S(2)}) collective-permute-start(f32[128,128]{1,0:T(8,128)S(1)} %collective-permute-done.12), channel_id=1, source_target_pairs={{0,15},{1,0},{2,1},{3,2},{4,3},{5,4},{6,5},{7,6},{8,7},{9,8},{10,9... | collective-permute-start | bytes 196616 | tf_op jit(solution)/shard_map/ppermute | solution.py:25
  65.2 44.8 %collective-permute-start.17 = (f32[128,128]{1,0:T(8,128)}, f32[128,128]{1,0:T(8,128)}, u32[]{:S(2)}, u32[]{:S(2)}) collective-permute-start(f32[128,128]{1,0:T(8,128)} %collective-permute-done.15), channel_id=1, source_target_pairs={{0,15},{1,0},{2,1},{3,2},{4,3},{5,4},{6,5},{7,6},{8,7},{9,8},{10,9... | collective-permute-start | bytes 196616 | tf_op jit(solution)/shard_map/ppermute | solution.py:25
  67.8 40.7 %collective-permute-start.16 = (f32[128,128]{1,0:T(8,128)S(1)}, f32[128,128]{1,0:T(8,128)S(1)}, u32[]{:S(2)}, u32[]{:S(2)}) collective-permute-start(f32[128,128]{1,0:T(8,128)S(1)} %collective-permute-done.14), channel_id=1, source_target_pairs={{0,15},{1,0},{2,1},{3,2},{4,3},{5,4},{6,5},{7,6},{8,7},{9,8},{10,9... | collective-permute-start | bytes 196616 | tf_op jit(solution)/shard_map/ppermute | solution.py:25
  100.1 17.1 %collective-permute-start.23 = (f32[128,128]{1,0:T(8,128)}, f32[128,128]{1,0:T(8,128)}, u32[]{:S(2)}, u32[]{:S(2)}) collective-permute-start(f32[128,128]{1,0:T(8,128)} %convolution_bitcast_fusion.11), channel_id=1, source_target_pairs={{0,15},{1,0},{2,1},{3,2},{4,3},{5,4},{6,5},{7,6},{8,7},{9,8},{10,9... | collective-permute-start | bytes 196616 | tf_op jit(solution)/shard_map/ppermute | solution.py:25
  103.1 15.6 %collective-permute-start.18 = (f32[128,128]{1,0:T(8,128)}, f32[128,128]{1,0:T(8,128)}, u32[]{:S(2)}, u32[]{:S(2)}) collective-permute-start(f32[128,128]{1,0:T(8,128)} %fusion.54), channel_id=1, source_target_pairs={{0,15},{1,0},{2,1},{3,2},{4,3},{5,4},{6,5},{7,6},{8,7},{9,8},{10,9... | collective-permute-start | bytes 196616 | tf_op jit(solution)/shard_map/ppermute | solution.py:25
  118.4 4.7 %collective-permute-start.24 = (f32[128,128]{1,0:T(8,128)S(1)}, f32[128,128]{1,0:T(8,128)S(1)}, u32[]{:S(2)}, u32[]{:S(2)}) collective-permute-start(f32[128,128]{1,0:T(8,128)S(1)} %fusion.56), channel_id=1, source_target_pairs={{0,15},{1,0},{2,1},{3,2},{4,3},{5,4},{6,5},{7,6},{8,7},{9,8},{10,9... | collective-permute-start | bytes 196616 | tf_op jit(solution)/shard_map/ppermute | solution.py:25
  120.0 4.4 %collective-permute-start.19 = (f32[128,128]{1,0:T(8,128)S(1)}, f32[128,128]{1,0:T(8,128)S(1)}, u32[]{:S(2)}, u32[]{:S(2)}) collective-permute-start(f32[128,128]{1,0:T(8,128)S(1)} %fusion.55), channel_id=1, source_target_pairs={{0,15},{1,0},{2,1},{3,2},{4,3},{5,4},{6,5},{7,6},{8,7},{9,8},{10,9... | collective-permute-start | bytes 196616 | tf_op jit(solution)/shard_map/ppermute | solution.py:25
  123.2 4.5 %collective-permute-start.25 = (f32[128,128]{1,0:T(8,128)S(1)}, f32[128,128]{1,0:T(8,128)S(1)}, u32[]{:S(2)}, u32[]{:S(2)}) collective-permute-start(f32[128,128]{1,0:T(8,128)S(1)} %add.353), channel_id=1, source_target_pairs={{0,15},{1,0},{2,1},{3,2},{4,3},{5,4},{6,5},{7,6},{8,7},{9,8},{10,9... | collective-permute-start | bytes 196616 | tf_op jit(solution)/shard_map/ppermute | solution.py:25
  124.4 5.3 %collective-permute-start.20 = (f32[128,128]{1,0:T(8,128)S(1)}, f32[128,128]{1,0:T(8,128)S(1)}, u32[]{:S(2)}, u32[]{:S(2)}) collective-permute-start(f32[128,128]{1,0:T(8,128)S(1)} %add.347), channel_id=1, source_target_pairs={{0,15},{1,0},{2,1},{3,2},{4,3},{5,4},{6,5},{7,6},{8,7},{9,8},{10,9... | collective-permute-start | bytes 196616 | tf_op jit(solution)/shard_map/ppermute | solution.py:25
  127.7 75.7 %collective-permute-start.26 = (f32[128,128]{1,0:T(8,128)S(1)}, f32[128,128]{1,0:T(8,128)S(1)}, u32[]{:S(2)}, u32[]{:S(2)}) collective-permute-start(f32[128,128]{1,0:T(8,128)S(1)} %add.354), channel_id=1, source_target_pairs={{0,15},{1,0},{2,1},{3,2},{4,3},{5,4},{6,5},{7,6},{8,7},{9,8},{10,9... | collective-permute-start | bytes 196616 | tf_op jit(solution)/shard_map/ppermute | solution.py:25
  129.7 75.3 %collective-permute-start.21 = (f32[128,128]{1,0:T(8,128)S(1)}, f32[128,128]{1,0:T(8,128)S(1)}, u32[]{:S(2)}, u32[]{:S(2)}) collective-permute-start(f32[128,128]{1,0:T(8,128)S(1)} %add.348), channel_id=1, source_target_pairs={{0,15},{1,0},{2,1},{3,2},{4,3},{5,4},{6,5},{7,6},{8,7},{9,8},{10,9... | collective-permute-start | bytes 196616 | tf_op jit(solution)/shard_map/ppermute | solution.py:25
  203.5 4.3 %collective-permute-start.27 = (f32[128,64]{1,0:T(8,128)S(1)}, f32[128,64]{1,0:T(8,128)S(1)}, u32[]{:S(2)}, u32[]{:S(2)}) collective-permute-start(f32[128,64]{1,0:T(8,128)S(1)} %slice_select_fusion), channel_id=1, source_target_pairs={{0,16},{16,0},{1,17},{17,1},{2,18},{18,2},{3,19},{19,3},{4,20},{20... | collective-permute-start | bytes 98312 | tf_op jit(solution)/shard_map/ppermute | solution.py:14
  205.1 4.3 %collective-permute-start.22 = (f32[128,64]{1,0:T(8,128)S(1)}, f32[128,64]{1,0:T(8,128)S(1)}, u32[]{:S(2)}, u32[]{:S(2)}) collective-permute-start(f32[128,64]{1,0:T(8,128)S(1)} %slice_select_fusion.1), channel_id=1, source_target_pairs={{0,16},{16,0},{1,17},{17,1},{2,18},{18,2},{3,19},{19,3},{4,20},{20... | collective-permute-start | bytes 98312 | tf_op jit(solution)/shard_map/ppermute | solution.py:14
  (15 other events, 135.9 us)
Sparse Core Ops, SparseCore 0:
  13.8 40.5 all-gather.2
  56.6 37.5 all-gather.4
  112.4 90.8 all-reduce.2
